TPU v7x, 32 devices: a whole 2x2x4 slice. The times are simulated.
32 devices in a mesh: row: 4 (over y, core), col: 8 (over z, x).
Axes of the slice: x: 2, y: 2, z: 4, core: 2. Of those that a mesh axis runs over, the one named last changes fastest.
Arguments:
- blocks: float32 [4096, 128, 128], P(('row', 'col')), may hold values from -0.25 to 0.25
- block_rows: int32 [32, 128], P(('row', 'col')), may hold values from 0 to 1023, as said below
- block_cols: int32 [32, 128], P(('row', 'col')), may hold values from 0 to 511
- diagonal: float32 [524288], P(('row', 'col')), may hold values from 1 to 4
- right_sides: float32 [2, 524288], P(None, ('row', 'col')), may hold values from -6 to 6
Outputs:
- solution: float32 [2, 524288], P(None, ('row', 'col'))
- hessenberg: float32 [2, 9, 8], replicated
Inputs may be any that keep to these rules, and one draw needn't show every extreme that they name: `block_rows`: non-decreasing along each tile's slots; a local block row may hold no stored block.
All inputs are finite; a program needn't handle non-finite values.
Results may differ from a plain program's by a relative error of at most 0.0085.
Values sent between devices are 32-bit elements; how exact they have to be, the bound alone decides.
A program may use at most 128 MiB of HBM per device.

v0:
```python
import jax
import jax.numpy as jnp
from jax import lax
from jax.sharding import PartitionSpec as P

STEPS = 8
epsilon = 1e-06


def least_squares(hessenberg, initial_norm):
    total_steps = hessenberg.shape[2]
    targets = [initial_norm] + [jnp.zeros_like(initial_norm) for j in range(total_steps)]
    cosines, sines, triangle = ([], [], [])
    for j in range(total_steps):
        column = [hessenberg[:, i, j] for i in range(j + 2)]
        for i in range(j):
            leading, trailing = (column[i], column[i + 1])
            column[i] = cosines[i] * leading + sines[i] * trailing
            column[i + 1] = cosines[i] * trailing - sines[i] * leading
        radius = jnp.sqrt(column[j] * column[j] + column[j + 1] * column[j + 1])
        cosine = column[j] / radius
        sine_term = column[j + 1] / radius
        column[j] = radius
        cosines.append(cosine)
        sines.append(sine_term)
        targets[j + 1] = -sine_term * targets[j]
        targets[j] = cosine * targets[j]
        triangle.append(column[: j + 1])
    coeffs = [None] * total_steps
    for j in reversed(range(total_steps)):
        running = targets[j]
        for k in range(j + 1, total_steps):
            running = running - triangle[k][j] * coeffs[k]
        coeffs[j] = running / triangle[j][j]
    return jnp.stack(coeffs, axis=1)


def apply_matrix(vector, blocks, rows_onehot, block_cols, diagonal):
    systems = vector.shape[0]
    width = blocks.shape[1]
    gathered = lax.all_gather(vector, "row", axis=1, tiled=True)
    grouped = gathered.reshape(systems, -1, width)
    picked = jnp.take(grouped, block_cols, axis=1)
    products = jnp.einsum("kij,nkj->nki", blocks, picked, precision=lax.Precision.HIGHEST)
    own_rows = lax.psum_scatter(
        jnp.einsum("mk,nki->mni", rows_onehot, products, precision=lax.Precision.HIGHEST),
        "col",
        scatter_dimension=0,
        tiled=True,
    )
    summed = jnp.transpose(own_rows, (1, 0, 2)).reshape(systems, -1)
    return diagonal[None, :] * vector + summed


def body(blocks, block_rows, block_cols, diagonal, right_sides):
    systems = right_sides.shape[0]
    width = blocks.shape[1]
    row_count = lax.axis_size("col") * (right_sides.shape[1] // width)
    positions = jnp.arange(row_count, dtype=jnp.int32)
    rows_onehot = (block_rows[0][None, :] == positions[:, None]).astype(jnp.float32)
    columns_local = block_cols[0]
    total_steps = STEPS
    initial_norm = jnp.sqrt(
        lax.psum(jnp.sum(right_sides * right_sides, axis=1), ("row", "col")) + epsilon
    )
    krylov_basis = [right_sides / initial_norm[:, None]]
    hessenberg = jnp.zeros((systems, total_steps + 1, total_steps), jnp.float32)
    for j in range(total_steps):
        candidate = apply_matrix(krylov_basis[j], blocks, rows_onehot, columns_local, diagonal)
        stacked = jnp.stack(krylov_basis)
        local_dots = jnp.einsum("inl,nl->ni", stacked, candidate, precision=lax.Precision.HIGHEST)
        coeffs = lax.psum(local_dots, ("row", "col"))
        candidate = candidate - jnp.einsum(
            "ni,inl->nl", coeffs, stacked, precision=lax.Precision.HIGHEST
        )
        remainder_sq = lax.psum(jnp.sum(candidate * candidate, axis=1), ("row", "col"))
        new_norm = jnp.sqrt(remainder_sq + epsilon)
        hessenberg = hessenberg.at[:, : j + 1, j].set(coeffs)
        hessenberg = hessenberg.at[:, j + 1, j].set(new_norm)
        krylov_basis.append(candidate / new_norm[:, None])
    weights = least_squares(hessenberg, initial_norm)
    solution = jnp.einsum(
        "ni,inl->nl",
        weights,
        jnp.stack(krylov_basis[:total_steps]),
        precision=lax.Precision.HIGHEST,
    )
    return (solution, hessenberg)


def solution(mesh):
    return jax.shard_map(
        body,
        mesh=mesh,
        in_specs=(
            P(("row", "col"), None, None),
            P(("row", "col"), None),
            P(("row", "col"), None),
            P(("row", "col")),
            P(None, ("row", "col")),
        ),
        out_specs=(P(None, ("row", "col")), P()),
        check_vma=False,
    )
```

profile of v0, /device:TPU:0, one launch (start us, length us, event | category | flops | bytes accessed | tf_op | source)
XLA Modules:
  0.0 1472.0 jit_solution(12052770710032486379)
XLA Ops:
  9.7 41.9 %psum.119 = f32[2]{0:T(128)S(1)} all-reduce(f32[2]{0:T(128)S(1)} %multiply_reduce_fusion.8), channel_id=1, replica_groups=mesh['row'=4,'col'=8] {'row','col'}, use_global_device_ids=true, to_apply=%region_1.0 | all-reduce | flops 2 | bytes 16 | tf_op jit(solution)/shard_map/psum | solution.py:64
  52.7 7.9 all_gather.24
  61.4 15.5 %convolution_bitcast_fusion.7 = f32[2,128,128]{2,0,1:T(2,128)S(1)} fusion(f32[128,128,128]{2,1,0:T(8,128)} %param.39, f32[128,2,128]{2,1,0:T(2,128)S(1)} %gather_fusion, pred[128]{0:T(512)(128)(4,1)S(1)} %compare_and_fusion), kind=kOutput, calls=%fused_computation.19 | convolution fusion | flops 50364416 | bytes 8650880 | tf_op jit(solution)/shard_map/kij,nkj->nki/dot_general | solution.py:44
  76.9 1.6 fusion.37
  79.3 62.7 %reduce-scatter.9.cloned.1.call-done = f32[128,2,128]{2,0,1:T(8,128)} async-done(((f32[1024,2,128]{2,0,1:T(8,128)}), f32[128,2,128]{2,0,1:T(8,128)}) %reduce-scatter.9.cloned.1.call-update) | async-done | bytes 131088 | tf_op jit(solution)/shard_map/reduce_scatter | solution.py:45
  143.1 39.9 %psum.120 = f32[2,1]{0,1:T(1,128)S(1)} all-reduce(f32[2,1]{0,1:T(1,128)S(1)} %bitcast.742), channel_id=1, replica_groups=mesh['row'=4,'col'=8] {'row','col'}, use_global_device_ids=true, to_apply=%region_3.5 | all-reduce | flops 2 | bytes 16 | tf_op jit(solution)/shard_map/psum | solution.py:72
  184.2 39.2 %psum.121 = f32[2]{0:T(128)S(1)} all-reduce(f32[2]{0:T(128)S(1)} %get-tuple-element.266), channel_id=1, replica_groups=mesh['row'=4,'col'=8] {'row','col'}, use_global_device_ids=true, to_apply=%region_5.7 | all-reduce | flops 2 | bytes 16 | tf_op jit(solution)/shard_map/psum | solution.py:76
  223.6 8.1 all_gather.25
  232.5 15.5 %convolution_bitcast_fusion.6 = f32[2,128,128]{2,0,1:T(2,128)S(1)} fusion(f32[128,128,128]{2,1,0:T(8,128)} %param.39, f32[128,2,128]{2,1,0:T(2,128)S(1)} %gather_fusion.1, pred[128]{0:T(512)(128)(4,1)S(1)} %compare_and_fusion), kind=kOutput, calls=%fused_computation.18 | convolution fusion | flops 50364416 | bytes 8650880 | tf_op jit(solution)/shard_map/kij,nkj->nki/dot_general | solution.py:44
  248.0 1.6 fusion.35
  251.0 61.7 %reduce-scatter.11.cloned.1.call-done = f32[128,2,128]{2,0,1:T(8,128)} async-done(((f32[1024,2,128]{2,0,1:T(8,128)}), f32[128,2,128]{2,0,1:T(8,128)}) %reduce-scatter.11.cloned.1.call-update) | async-done | bytes 131088 | tf_op jit(solution)/shard_map/reduce_scatter | solution.py:45
  313.8 2.5 fusion.53
  316.2 39.8 %psum.122 = f32[2,2]{1,0:T(2,128)S(1)} all-reduce(f32[2,2]{1,0:T(2,128)S(1)} %bitcast.732), channel_id=1, replica_groups=mesh['row'=4,'col'=8] {'row','col'}, use_global_device_ids=true, to_apply=%region_7.9 | all-reduce | flops 4 | bytes 32 | tf_op jit(solution)/shard_map/psum | solution.py:72
  357.4 39.2 %psum.123 = f32[2]{0:T(128)S(1)} all-reduce(f32[2]{0:T(128)S(1)} %multiply_reduce_fusion.6), channel_id=1, replica_groups=mesh['row'=4,'col'=8] {'row','col'}, use_global_device_ids=true, to_apply=%region_9.11 | all-reduce | flops 2 | bytes 16 | tf_op jit(solution)/shard_map/psum | solution.py:76
  396.8 8.2 all_gather.26
  406.4 15.5 %convolution_bitcast_fusion.5 = f32[2,128,128]{2,0,1:T(2,128)S(1)} fusion(f32[128,128,128]{2,1,0:T(8,128)} %param.39, f32[128,2,128]{2,1,0:T(2,128)} %gather_fusion.2, pred[128]{0:T(512)(128)(4,1)S(1)} %compare_and_fusion), kind=kOutput, calls=%fused_computation.17 | convolution fusion | flops 50364416 | bytes 8650880 | tf_op jit(solution)/shard_map/kij,nkj->nki/dot_general | solution.py:44
  421.9 1.6 fusion.33
  425.1 61.8 %reduce-scatter.13.cloned.1.call-done = f32[128,2,128]{2,0,1:T(8,128)} async-done(((f32[1024,2,128]{2,0,1:T(8,128)}), f32[128,2,128]{2,0,1:T(8,128)}) %reduce-scatter.13.cloned.1.call-update) | async-done | bytes 131088 | tf_op jit(solution)/shard_map/reduce_scatter | solution.py:45
  487.9 2.5 fusion.20
  490.4 39.8 %psum.124 = f32[2,3]{1,0:T(2,128)S(1)} all-reduce(f32[2,3]{1,0:T(2,128)S(1)} %bitcast.733), channel_id=1, replica_groups=mesh['row'=4,'col'=8] {'row','col'}, use_global_device_ids=true, to_apply=%region_12.14 | all-reduce | flops 6 | bytes 48 | tf_op jit(solution)/shard_map/psum | solution.py:72
  532.7 39.2 %psum.125 = f32[2]{0:T(128)S(1)} all-reduce(f32[2]{0:T(128)S(1)} %multiply_reduce_fusion.5), channel_id=1, replica_groups=mesh['row'=4,'col'=8] {'row','col'}, use_global_device_ids=true, to_apply=%region_14.16 | all-reduce | flops 2 | bytes 16 | tf_op jit(solution)/shard_map/psum | solution.py:76
  573.0 8.8 all_gather.27
  581.8 1.8 gather_fusion.3
  583.6 15.5 %convolution_bitcast_fusion.4 = f32[2,128,128]{2,0,1:T(2,128)S(1)} fusion(f32[128,128,128]{2,1,0:T(8,128)} %param.39, f32[128,2,128]{2,1,0:T(2,128)S(1)} %gather_fusion.3, pred[128]{0:T(512)(128)(4,1)S(1)} %compare_and_fusion), kind=kOutput, calls=%fused_computation.16 | convolution fusion | flops 50364416 | bytes 8650880 | tf_op jit(solution)/shard_map/kij,nkj->nki/dot_general | solution.py:44
  599.1 1.6 fusion.31
  602.6 61.4 %reduce-scatter.15.cloned.1.call-done = f32[128,2,128]{2,0,1:T(8,128)} async-done(((f32[1024,2,128]{2,0,1:T(8,128)}), f32[128,2,128]{2,0,1:T(8,128)}) %reduce-scatter.15.cloned.1.call-update) | async-done | bytes 131088 | tf_op jit(solution)/shard_map/reduce_scatter | solution.py:45
  665.0 3.6 fusion.41
  668.6 39.8 %psum.126 = f32[2,4]{1,0:T(2,128)S(1)} all-reduce(f32[2,4]{1,0:T(2,128)S(1)} %bitcast.734), channel_id=1, replica_groups=mesh['row'=4,'col'=8] {'row','col'}, use_global_device_ids=true, to_apply=%region_17.19 | all-reduce | flops 8 | bytes 64 | tf_op jit(solution)/shard_map/psum | solution.py:72
  708.5 2.3 fusion.39
  712.2 39.1 %psum.127 = f32[2]{0:T(128)S(1)} all-reduce(f32[2]{0:T(128)S(1)} %multiply_reduce_fusion.4), channel_id=1, replica_groups=mesh['row'=4,'col'=8] {'row','col'}, use_global_device_ids=true, to_apply=%region_19.21 | all-reduce | flops 2 | bytes 16 | tf_op jit(solution)/shard_map/psum | solution.py:76
  753.1 8.6 all_gather.28
  761.7 2.4 gather_fusion.4
  764.1 15.5 %convolution_bitcast_fusion.3 = f32[2,128,128]{2,0,1:T(2,128)S(1)} fusion(f32[128,128,128]{2,1,0:T(8,128)} %param.39, f32[128,2,128]{2,1,0:T(2,128)} %gather_fusion.4, pred[128]{0:T(512)(128)(4,1)S(1)} %compare_and_fusion), kind=kOutput, calls=%fused_computation.15 | convolution fusion | flops 50364416 | bytes 8650880 | tf_op jit(solution)/shard_map/kij,nkj->nki/dot_general | solution.py:44
  782.3 62.2 %reduce-scatter.17.cloned.1.call-done = f32[128,2,128]{2,0,1:T(8,128)} async-done(((f32[1024,2,128]{2,0,1:T(8,128)}), f32[128,2,128]{2,0,1:T(8,128)}) %reduce-scatter.17.cloned.1.call-update) | async-done | bytes 131088 | tf_op jit(solution)/shard_map/reduce_scatter | solution.py:45
  846.3 2.6 fusion.2
  848.9 39.8 %psum.128 = f32[2,5]{1,0:T(2,128)S(1)} all-reduce(f32[2,5]{1,0:T(2,128)S(1)} %bitcast.727), channel_id=1, replica_groups=mesh['row'=4,'col'=8] {'row','col'}, use_global_device_ids=true, to_apply=%region_22.24 | all-reduce | flops 10 | bytes 80 | tf_op jit(solution)/shard_map/psum | solution.py:72
  891.8 39.3 %psum.129 = f32[2]{0:T(128)S(1)} all-reduce(f32[2]{0:T(128)S(1)} %multiply_reduce_fusion.3), channel_id=1, replica_groups=mesh['row'=4,'col'=8] {'row','col'}, use_global_device_ids=true, to_apply=%region_24.26 | all-reduce | flops 2 | bytes 16 | tf_op jit(solution)/shard_map/psum | solution.py:76
  932.3 8.2 all_gather.29
  941.8 15.5 %convolution_bitcast_fusion.2 = f32[2,128,128]{2,0,1:T(2,128)S(1)} fusion(f32[128,128,128]{2,1,0:T(8,128)} %param.39, f32[128,2,128]{2,1,0:T(2,128)} %gather_fusion.5, pred[128]{0:T(512)(128)(4,1)S(1)} %compare_and_fusion), kind=kOutput, calls=%fused_computation.14 | convolution fusion | flops 50364416 | bytes 8650880 | tf_op jit(solution)/shard_map/kij,nkj->nki/dot_general | solution.py:44
  957.3 1.6 fusion.27
  959.1 63.2 %reduce-scatter.19.cloned.1.call-done = f32[128,2,128]{2,0,1:T(8,128)} async-done(((f32[1024,2,128]{2,0,1:T(8,128)}), f32[128,2,128]{2,0,1:T(8,128)}) %reduce-scatter.19.cloned.1.call-update) | async-done | bytes 131088 | tf_op jit(solution)/shard_map/reduce_scatter | solution.py:45
  1023.3 2.9 fusion.6
  1026.2 39.8 %psum.130 = f32[2,6]{1,0:T(2,128)S(1)} all-reduce(f32[2,6]{1,0:T(2,128)S(1)} %bitcast.728), channel_id=1, replica_groups=mesh['row'=4,'col'=8] {'row','col'}, use_global_device_ids=true, to_apply=%region_27.29 | all-reduce | flops 12 | bytes 96 | tf_op jit(solution)/shard_map/psum | solution.py:72
  1068.3 39.2 %psum.131 = f32[2]{0:T(128)S(1)} all-reduce(f32[2]{0:T(128)S(1)} %multiply_reduce_fusion.2), channel_id=1, replica_groups=mesh['row'=4,'col'=8] {'row','col'}, use_global_device_ids=true, to_apply=%region_29.31 | all-reduce | flops 2 | bytes 16 | tf_op jit(solution)/shard_map/psum | solution.py:76
  1107.7 8.4 all_gather.30
  1116.8 15.5 %convolution_bitcast_fusion.1 = f32[2,128,128]{2,0,1:T(2,128)S(1)} fusion(f32[128,128,128]{2,1,0:T(8,128)} %param.39, f32[128,2,128]{2,1,0:T(2,128)S(1)} %gather_fusion.6, pred[128]{0:T(512)(128)(4,1)S(1)} %compare_and_fusion), kind=kOutput, calls=%fused_computation.13 | convolution fusion | flops 50364416 | bytes 8650880 | tf_op jit(solution)/shard_map/kij,nkj->nki/dot_general | solution.py:44
  1132.3 1.6 fusion.25
  1134.0 63.2 %reduce-scatter.21.cloned.1.call-done = f32[128,2,128]{2,0,1:T(8,128)} async-done(((f32[1024,2,128]{2,0,1:T(8,128)}), f32[128,2,128]{2,0,1:T(8,128)}) %reduce-scatter.21.cloned.1.call-update) | async-done | bytes 131088 | tf_op jit(solution)/shard_map/reduce_scatter | solution.py:45
  1198.3 2.9 fusion.10
  1201.2 39.9 %psum.132 = f32[2,7]{1,0:T(2,128)S(1)} all-reduce(f32[2,7]{1,0:T(2,128)S(1)} %bitcast.729), channel_id=1, replica_groups=mesh['row'=4,'col'=8] {'row','col'}, use_global_device_ids=true, to_apply=%region_32.34 | all-reduce | flops 14 | bytes 112 | tf_op jit(solution)/shard_map/psum | solution.py:72
  1242.8 39.2 %psum.133 = f32[2]{0:T(128)S(1)} all-reduce(f32[2]{0:T(128)S(1)} %multiply_reduce_fusion.1), channel_id=1, replica_groups=mesh['row'=4,'col'=8] {'row','col'}, use_global_device_ids=true, to_apply=%region_34.36 | all-reduce | flops 2 | bytes 16 | tf_op jit(solution)/shard_map/psum | solution.py:76
  1282.2 8.1 all_gather.31
  1291.1 15.5 %convolution_bitcast_fusion = f32[2,128,128]{2,0,1:T(2,128)S(1)} fusion(f32[128,128,128]{2,1,0:T(8,128)} %param.39, f32[128,2,128]{2,1,0:T(2,128)S(1)} %gather_fusion.7, pred[128]{0:T(512)(128)(4,1)S(1)} %compare_and_fusion), kind=kOutput, calls=%fused_computation.12 | convolution fusion | flops 50364416 | bytes 8650880 | tf_op jit(solution)/shard_map/kij,nkj->nki/dot_general | solution.py:44
  1306.5 1.6 fusion.23
  1315.4 1.8 broadcast_select_fusion.5
  1318.6 2.0 broadcast_select_fusion.4
  1322.1 2.0 broadcast_select_fusion.3
  1325.6 1.9 broadcast_select_fusion.2
  1328.9 2.0 broadcast_select_fusion.1
  1332.2 39.3 %reduce-scatter.23.cloned.1.call-done = f32[128,2,128]{2,0,1:T(8,128)} async-done(((f32[1024,2,128]{2,0,1:T(8,128)}), f32[128,2,128]{2,0,1:T(8,128)}) %reduce-scatter.23.cloned.1.call-update) | async-done | bytes 131088 | tf_op jit(solution)/shard_map/reduce_scatter | solution.py:45
  1372.6 3.0 fusion.16
  1375.6 39.8 %psum.134 = f32[2,8]{1,0:T(2,128)S(1)} all-reduce(f32[2,8]{1,0:T(2,128)S(1)} %bitcast.726), channel_id=1, replica_groups=mesh['row'=4,'col'=8] {'row','col'}, use_global_device_ids=true, to_apply=%region_37.39 | all-reduce | flops 16 | bytes 128 | tf_op jit(solution)/shard_map/psum | solution.py:72
  1418.4 39.2 %psum.135 = f32[2]{0:T(128)S(1)} all-reduce(f32[2]{0:T(128)S(1)} %fusion.56), channel_id=1, replica_groups=mesh['row'=4,'col'=8] {'row','col'}, use_global_device_ids=true, to_apply=%region_39.41 | all-reduce | flops 2 | bytes 16 | tf_op jit(solution)/shard_map/psum | solution.py:76
  1457.7 1.8 broadcast_select_fusion
  (165 shorter events, 68.4 us)
Async XLA Ops:
  7.2 69.7 %copy-start.8 = (s32[1,128]{1,0:T(1,128)S(1)}, s32[1,128]{1,0:T(1,128)}, u32[]{:S(2)}) copy-start(s32[1,128]{1,0:T(1,128)} %param.40) | copy-start | bytes 1540
  7.2 134.8 %copy-start = (f32[16384]{0:T(1024)S(1)}, f32[16384]{0:T(1024)}, u32[]{:S(2)}) copy-start(f32[16384]{0:T(1024)} %param.42) | copy-start | bytes 196612
  7.2 134.8 %reduce-scatter.9.cloned.1.call-start = ((), (), s32[]{:S(2)}) async-start(), calls=%async_computation.8 | async-start | bytes 1179648 | tf_op jit(solution)/shard_map/reduce_scatter | solution.py:45
  78.5 234.2 %reduce-scatter.11.cloned.1.call-start = ((), (), s32[]{:S(2)}) async-start(), calls=%async_computation.9 | async-start | bytes 1179648 | tf_op jit(solution)/shard_map/reduce_scatter | solution.py:45
  249.6 237.3 %reduce-scatter.13.cloned.1.call-start = ((), (), s32[]{:S(2)}) async-start(), calls=%async_computation.10 | async-start | bytes 1179648 | tf_op jit(solution)/shard_map/reduce_scatter | solution.py:45
  423.5 240.4 %reduce-scatter.15.cloned.1.call-start = ((), (), s32[]{:S(2)}) async-start(), calls=%async_computation.11 | async-start | bytes 1179648 | tf_op jit(solution)/shard_map/reduce_scatter | solution.py:45
  531.3 0.7 copy-start.6
  600.7 243.8 %reduce-scatter.17.cloned.1.call-start = ((), (), s32[]{:S(2)}) async-start(), calls=%async_computation.12 | async-start | bytes 1179648 | tf_op jit(solution)/shard_map/reduce_scatter | solution.py:45
  665.0 46.0 %copy-start.4 = (f32[2,16384]{1,0:T(2,128)}, f32[2,16384]{1,0:T(2,128)S(1)}, u32[]{:S(2)}) copy-start(f32[2,16384]{1,0:T(2,128)S(1)} %bitcast_add_fusion.4) | copy-start | bytes 393220
  710.8 0.6 copy-start.5
  712.2 69.1 %copy-start.1 = (f32[7,2,16384]{2,1,0:T(2,128)S(1)}, f32[7,2,16384]{2,1,0:T(2,128)}, u32[]{:S(2)}) copy-start(f32[7,2,16384]{2,1,0:T(2,128)} %get-tuple-element.273) | copy-start | bytes 2752516
  752.5 0.7 copy-start.2
  781.2 241.0 %reduce-scatter.19.cloned.1.call-start = ((), (), s32[]{:S(2)}) async-start(), calls=%async_computation.13 | async-start | bytes 1179648 | tf_op jit(solution)/shard_map/reduce_scatter | solution.py:45
  845.6 0.7 copy-start.3
  890.0 0.6 copy-start.7
  958.9 238.3 %reduce-scatter.21.cloned.1.call-start = ((), (), s32[]{:S(2)}) async-start(), calls=%async_computation.14 | async-start | bytes 1179648 | tf_op jit(solution)/shard_map/reduce_scatter | solution.py:45
  1133.8 175.5 %copy-start.14 = (s32[3]{0:T(128)S(1)}, s32[3]{0:T(128)}, u32[]{:S(2)}) copy-start(s32[3]{0:T(128)} %constant.460.clone.1) | copy-start | bytes 40
  1133.9 176.2 %copy-start.13 = (s32[3]{0:T(128)S(1)}, s32[3]{0:T(128)}, u32[]{:S(2)}) copy-start(s32[3]{0:T(128)} %constant.463.clone.1) | copy-start | bytes 40
  1133.9 177.0 %copy-start.12 = (s32[3]{0:T(128)S(1)}, s32[3]{0:T(128)}, u32[]{:S(2)}) copy-start(s32[3]{0:T(128)} %constant.465.clone.1) | copy-start | bytes 40
  1133.9 177.7 %copy-start.11 = (s32[3]{0:T(128)S(1)}, s32[3]{0:T(128)}, u32[]{:S(2)}) copy-start(s32[3]{0:T(128)} %constant.467.clone.1) | copy-start | bytes 40
  1133.9 178.5 %copy-start.10 = (s32[3]{0:T(128)S(1)}, s32[3]{0:T(128)}, u32[]{:S(2)}) copy-start(s32[3]{0:T(128)} %constant.469.clone.1) | copy-start | bytes 40
  1133.9 179.2 %copy-start.9 = (s32[3]{0:T(128)S(1)}, s32[3]{0:T(128)}, u32[]{:S(2)}) copy-start(s32[3]{0:T(128)} %constant.471.clone.1) | copy-start | bytes 40
  1133.9 237.6 %reduce-scatter.23.cloned.1.call-start = ((), (), s32[]{:S(2)}) async-start(), calls=%async_computation.15 | async-start | bytes 1179648 | tf_op jit(solution)/shard_map/reduce_scatter | solution.py:45
Sparse Core Ops, SparseCore 0:
  78.6 63.3 reduce-scatter.8
  249.7 62.9 reduce-scatter.10
  423.6 63.1 reduce-scatter.12
  600.8 63.0 reduce-scatter.14
  781.3 63.1 reduce-scatter.16
  959.1 63.1 reduce-scatter.18
  1134.0 63.1 reduce-scatter.20
  1308.3 63.1 reduce-scatter.22
where the time goes:
time: 1480 us; the launch traced here: 1470 us
  blocking collectives  740 us (50%)
  waiting for transfers between devices  476 us (32%)
  matrix products  168 us (11%)
  other arithmetic  38.8 us (3%)
  local copies, waits for them, and re-layouts  33.9 us (2%)
  between operations  14.8 us (1%)
    reduce_scatter x8, waiting for transfers between devices, apply_matrix(): lax.psum_scatter(jnp.einsum('mk,nki->mni', rows_onehot, products, precisi...  475 us
    psum x8, blocking collectives, body(): coeffs = lax.psum(local_dots, ('row', 'col'))  319 us
    psum x8, blocking collectives, body(): lax.psum(jnp.sum(candidate * candidate, axis=1), ('row', 'col'))  314 us
    dot_general x8, matrix products, apply_matrix(): jnp.einsum('kij,nkj->nki', blocks, picked, precision=lax.Precision.HIGHEST)  124 us
    all_gather x8, blocking collectives, apply_matrix(): gathered = lax.all_gather(vector, 'row', axis=1, tiled=True)  66.2 us
    psum x1, blocking collectives, body(): lax.psum(jnp.sum(right_sides * right_sides, axis=1), ('row', 'col'))  41.9 us
  transfers between devices with their start and end apart: 8, of which 8 were waited for; matrix products, arithmetic and copies ran while one was open for 2% of the time, Pallas kernels for 0%

commit v1 on v0

--- a/solution.py
+++ b/solution.py
@@ -73,7 +73,9 @@
         candidate = candidate - jnp.einsum(
             "ni,inl->nl", coeffs, stacked, precision=lax.Precision.HIGHEST
         )
-        remainder_sq = lax.psum(jnp.sum(candidate * candidate, axis=1), ("row", "col"))
+        remainder_sq = jnp.sum(
+            lax.all_gather(jnp.sum(candidate * candidate, axis=1), ("row", "col")), axis=0
+        )
         new_norm = jnp.sqrt(remainder_sq + epsilon)
         hessenberg = hessenberg.at[:, : j + 1, j].set(coeffs)
         hessenberg = hessenberg.at[:, j + 1, j].set(new_norm)

time: 1480 us -> 1490 us (level)
    psum x8 -> x0, blocking collectives: 314 us -> none  [body(): lax.psum(jnp.sum(candidate * candidate, axis=1), ('row', 'col'))]
    unnamed x0 -> x8, blocking collectives: none -> 314 us
where the time goes in v1:
time: 1490 us; the launch traced here: 1480 us
  blocking collectives  741 us (50%)
  waiting for transfers between devices  473 us (32%)
  matrix products  168 us (11%)
  other arithmetic  42.3 us (3%)
  local copies, waits for them, and re-layouts  38.1 us (3%)
  between operations  15.2 us (1%)
    reduce_scatter x8, waiting for transfers between devices, apply_matrix(): lax.psum_scatter(jnp.einsum('mk,nki->mni', rows_onehot, products, precisi...  472 us
    psum x8, blocking collectives, body(): coeffs = lax.psum(local_dots, ('row', 'col'))  319 us
    unnamed x8, blocking collectives  314 us
    dot_general x8, matrix products, apply_matrix(): jnp.einsum('kij,nkj->nki', blocks, picked, precision=lax.Precision.HIGHEST)  124 us
    all_gather x8, blocking collectives, apply_matrix(): gathered = lax.all_gather(vector, 'row', axis=1, tiled=True)  66.5 us
    psum x1, blocking collectives, body(): lax.psum(jnp.sum(right_sides * right_sides, axis=1), ('row', 'col'))  41.9 us
  transfers between devices with their start and end apart: 8, of which 8 were waited for; matrix products, arithmetic and copies ran while one was open for 2% of the time, Pallas kernels for 0%

profile of v1, /device:TPU:0, one launch (start us, length us, event | category | flops | bytes accessed | tf_op | source)
XLA Modules:
  0.0 1477.4 jit_solution(2276228099475701489)
XLA Ops:
  9.7 41.9 %psum.63 = f32[2]{0:T(128)S(1)} all-reduce(f32[2]{0:T(128)S(1)} %multiply_reduce_fusion.8), channel_id=1, replica_groups=mesh['row'=4,'col'=8] {'row','col'}, use_global_device_ids=true, to_apply=%region_1.0 | all-reduce | flops 2 | bytes 16 | tf_op jit(solution)/shard_map/psum | solution.py:64
  52.7 7.9 all_gather.72
  61.4 15.5 %convolution_bitcast_fusion.7 = f32[2,128,128]{2,0,1:T(2,128)S(1)} fusion(f32[128,128,128]{2,1,0:T(8,128)} %param.39, f32[128,2,128]{2,1,0:T(2,128)S(1)} %gather_fusion, pred[128]{0:T(512)(128)(4,1)S(1)} %compare_and_fusion), kind=kOutput, calls=%fused_computation.19 | convolution fusion | flops 50364416 | bytes 8650880 | tf_op jit(solution)/shard_map/kij,nkj->nki/dot_general | solution.py:44
  76.9 1.6 fusion.37
  82.4 59.4 %reduce-scatter.9.cloned.1.call-done = f32[128,2,128]{2,0,1:T(8,128)} async-done(((f32[1024,2,128]{2,0,1:T(8,128)}), f32[128,2,128]{2,0,1:T(8,128)}) %reduce-scatter.9.cloned.1.call-update) | async-done | bytes 131088 | tf_op jit(solution)/shard_map/reduce_scatter | solution.py:45
  142.9 39.9 %psum.64 = f32[2,1]{0,1:T(1,128)S(1)} all-reduce(f32[2,1]{0,1:T(1,128)S(1)} %bitcast.742), channel_id=1, replica_groups=mesh['row'=4,'col'=8] {'row','col'}, use_global_device_ids=true, to_apply=%region_3.5 | all-reduce | flops 2 | bytes 16 | tf_op jit(solution)/shard_map/psum | solution.py:72
  184.3 39.2 %all-reduce.1 = f32[64]{0:T(128)S(1)} all-reduce(f32[64]{0:T(128)S(1)} %dynamic-update-slice.48), channel_id=2, replica_groups=mesh['row'=4,'col'=8] {'row','col'}, use_global_device_ids=true, to_apply=%add.1 | all-reduce | flops 64 | bytes 512
  223.8 8.2 all_gather.75
  232.7 15.5 %convolution_bitcast_fusion.6 = f32[2,128,128]{2,0,1:T(2,128)S(1)} fusion(f32[128,128,128]{2,1,0:T(8,128)} %param.39, f32[128,2,128]{2,1,0:T(2,128)S(1)} %gather_fusion.1, pred[128]{0:T(512)(128)(4,1)S(1)} %compare_and_fusion), kind=kOutput, calls=%fused_computation.18 | convolution fusion | flops 50364416 | bytes 8650880 | tf_op jit(solution)/shard_map/kij,nkj->nki/dot_general | solution.py:44
  248.1 1.6 fusion.35
  250.7 62.3 %reduce-scatter.11.cloned.1.call-done = f32[128,2,128]{2,0,1:T(8,128)} async-done(((f32[1024,2,128]{2,0,1:T(8,128)}), f32[128,2,128]{2,0,1:T(8,128)}) %reduce-scatter.11.cloned.1.call-update) | async-done | bytes 131088 | tf_op jit(solution)/shard_map/reduce_scatter | solution.py:45
  314.1 2.5 fusion.53
  316.6 39.8 %psum.65 = f32[2,2]{1,0:T(2,128)S(1)} all-reduce(f32[2,2]{1,0:T(2,128)S(1)} %bitcast.732), channel_id=1, replica_groups=mesh['row'=4,'col'=8] {'row','col'}, use_global_device_ids=true, to_apply=%region_7.9 | all-reduce | flops 4 | bytes 32 | tf_op jit(solution)/shard_map/psum | solution.py:72
  357.9 39.3 %all-reduce.2 = f32[64]{0:T(128)S(1)} all-reduce(f32[64]{0:T(128)S(1)} %dynamic-update-slice.49), channel_id=3, replica_groups=mesh['row'=4,'col'=8] {'row','col'}, use_global_device_ids=true, to_apply=%add.2 | all-reduce | flops 64 | bytes 512
  397.5 8.4 all_gather.78
  407.3 15.5 %convolution_bitcast_fusion.5 = f32[2,128,128]{2,0,1:T(2,128)S(1)} fusion(f32[128,128,128]{2,1,0:T(8,128)} %param.39, f32[128,2,128]{2,1,0:T(2,128)} %gather_fusion.2, pred[128]{0:T(512)(128)(4,1)S(1)} %compare_and_fusion), kind=kOutput, calls=%fused_computation.17 | convolution fusion | flops 50364416 | bytes 8650880 | tf_op jit(solution)/shard_map/kij,nkj->nki/dot_general | solution.py:44
  422.8 1.6 fusion.33
  425.4 62.3 %reduce-scatter.13.cloned.1.call-done = f32[128,2,128]{2,0,1:T(8,128)} async-done(((f32[1024,2,128]{2,0,1:T(8,128)}), f32[128,2,128]{2,0,1:T(8,128)}) %reduce-scatter.13.cloned.1.call-update) | async-done | bytes 131088 | tf_op jit(solution)/shard_map/reduce_scatter | solution.py:45
  488.8 2.5 fusion.20
  491.2 39.8 %psum.66 = f32[2,3]{1,0:T(2,128)S(1)} all-reduce(f32[2,3]{1,0:T(2,128)S(1)} %bitcast.733), channel_id=1, replica_groups=mesh['row'=4,'col'=8] {'row','col'}, use_global_device_ids=true, to_apply=%region_12.14 | all-reduce | flops 6 | bytes 48 | tf_op jit(solution)/shard_map/psum | solution.py:72
  533.3 39.2 %all-reduce.3 = f32[64]{0:T(128)S(1)} all-reduce(f32[64]{0:T(128)S(1)} %dynamic-update-slice.50), channel_id=4, replica_groups=mesh['row'=4,'col'=8] {'row','col'}, use_global_device_ids=true, to_apply=%add.3 | all-reduce | flops 64 | bytes 512
  573.8 8.6 all_gather.81
  582.3 1.8 gather_fusion.3
  584.1 15.5 %convolution_bitcast_fusion.4 = f32[2,128,128]{2,0,1:T(2,128)S(1)} fusion(f32[128,128,128]{2,1,0:T(8,128)} %param.39, f32[128,2,128]{2,1,0:T(2,128)S(1)} %gather_fusion.3, pred[128]{0:T(512)(128)(4,1)S(1)} %compare_and_fusion), kind=kOutput, calls=%fused_computation.16 | convolution fusion | flops 50364416 | bytes 8650880 | tf_op jit(solution)/shard_map/kij,nkj->nki/dot_general | solution.py:44
  599.6 1.6 fusion.31
  603.1 61.4 %reduce-scatter.15.cloned.1.call-done = f32[128,2,128]{2,0,1:T(8,128)} async-done(((f32[1024,2,128]{2,0,1:T(8,128)}), f32[128,2,128]{2,0,1:T(8,128)}) %reduce-scatter.15.cloned.1.call-update) | async-done | bytes 131088 | tf_op jit(solution)/shard_map/reduce_scatter | solution.py:45
  666.3 3.6 fusion.41
  669.8 39.8 %psum.67 = f32[2,4]{1,0:T(2,128)S(1)} all-reduce(f32[2,4]{1,0:T(2,128)S(1)} %bitcast.734), channel_id=1, replica_groups=mesh['row'=4,'col'=8] {'row','col'}, use_global_device_ids=true, to_apply=%region_17.19 | all-reduce | flops 8 | bytes 64 | tf_op jit(solution)/shard_map/psum | solution.py:72
  709.6 2.3 fusion.39
  714.0 39.2 %all-reduce.4 = f32[64]{0:T(128)} all-reduce(f32[64]{0:T(128)S(1)} %dynamic-update-slice.51), channel_id=5, replica_groups=mesh['row'=4,'col'=8] {'row','col'}, use_global_device_ids=true, to_apply=%add.4 | all-reduce | flops 64 | bytes 512
  757.4 8.8 all_gather.84
  766.2 2.4 gather_fusion.4
  768.6 15.5 %convolution_bitcast_fusion.3 = f32[2,128,128]{2,0,1:T(2,128)S(1)} fusion(f32[128,128,128]{2,1,0:T(8,128)} %param.39, f32[128,2,128]{2,1,0:T(2,128)} %gather_fusion.4, pred[128]{0:T(512)(128)(4,1)S(1)} %compare_and_fusion), kind=kOutput, calls=%fused_computation.15 | convolution fusion | flops 50364416 | bytes 8650880 | tf_op jit(solution)/shard_map/kij,nkj->nki/dot_general | solution.py:44
  784.1 1.6 fusion.29
  786.8 61.9 %reduce-scatter.17.cloned.1.call-done = f32[128,2,128]{2,0,1:T(8,128)} async-done(((f32[1024,2,128]{2,0,1:T(8,128)}), f32[128,2,128]{2,0,1:T(8,128)}) %reduce-scatter.17.cloned.1.call-update) | async-done | bytes 131088 | tf_op jit(solution)/shard_map/reduce_scatter | solution.py:45
  850.6 2.6 fusion.2
  853.2 39.8 %psum.68 = f32[2,5]{1,0:T(2,128)S(1)} all-reduce(f32[2,5]{1,0:T(2,128)S(1)} %bitcast.727), channel_id=1, replica_groups=mesh['row'=4,'col'=8] {'row','col'}, use_global_device_ids=true, to_apply=%region_22.24 | all-reduce | flops 10 | bytes 80 | tf_op jit(solution)/shard_map/psum | solution.py:72
  896.4 39.2 %all-reduce.5 = f32[64]{0:T(128)S(1)} all-reduce(f32[64]{0:T(128)S(1)} %dynamic-update-slice.52), channel_id=6, replica_groups=mesh['row'=4,'col'=8] {'row','col'}, use_global_device_ids=true, to_apply=%add.5 | all-reduce | flops 64 | bytes 512
  937.4 8.4 all_gather.87
  947.2 15.5 %convolution_bitcast_fusion.2 = f32[2,128,128]{2,0,1:T(2,128)S(1)} fusion(f32[128,128,128]{2,1,0:T(8,128)} %param.39, f32[128,2,128]{2,1,0:T(2,128)} %gather_fusion.5, pred[128]{0:T(512)(128)(4,1)S(1)} %compare_and_fusion), kind=kOutput, calls=%fused_computation.14 | convolution fusion | flops 50364416 | bytes 8650880 | tf_op jit(solution)/shard_map/kij,nkj->nki/dot_general | solution.py:44
  964.4 63.1 %reduce-scatter.19.cloned.1.call-done = f32[128,2,128]{2,0,1:T(8,128)} async-done(((f32[1024,2,128]{2,0,1:T(8,128)}), f32[128,2,128]{2,0,1:T(8,128)}) %reduce-scatter.19.cloned.1.call-update) | async-done | bytes 131088 | tf_op jit(solution)/shard_map/reduce_scatter | solution.py:45
  1028.6 2.9 fusion.6
  1031.5 39.8 %psum.69 = f32[2,6]{1,0:T(2,128)S(1)} all-reduce(f32[2,6]{1,0:T(2,128)S(1)} %bitcast.728), channel_id=1, replica_groups=mesh['row'=4,'col'=8] {'row','col'}, use_global_device_ids=true, to_apply=%region_27.29 | all-reduce | flops 12 | bytes 96 | tf_op jit(solution)/shard_map/psum | solution.py:72
  1073.2 39.2 %all-reduce.6 = f32[64]{0:T(128)S(1)} all-reduce(f32[64]{0:T(128)S(1)} %dynamic-update-slice.53), channel_id=7, replica_groups=mesh['row'=4,'col'=8] {'row','col'}, use_global_device_ids=true, to_apply=%add.6 | all-reduce | flops 64 | bytes 512
  1112.7 8.1 all_gather.90
  1121.6 15.5 %convolution_bitcast_fusion.1 = f32[2,128,128]{2,0,1:T(2,128)S(1)} fusion(f32[128,128,128]{2,1,0:T(8,128)} %param.39, f32[128,2,128]{2,1,0:T(2,128)S(1)} %gather_fusion.6, pred[128]{0:T(512)(128)(4,1)S(1)} %compare_and_fusion), kind=kOutput, calls=%fused_computation.13 | convolution fusion | flops 50364416 | bytes 8650880 | tf_op jit(solution)/shard_map/kij,nkj->nki/dot_general | solution.py:44
  1137.0 1.6 fusion.25
  1138.8 63.2 %reduce-scatter.21.cloned.1.call-done = f32[128,2,128]{2,0,1:T(8,128)} async-done(((f32[1024,2,128]{2,0,1:T(8,128)}), f32[128,2,128]{2,0,1:T(8,128)}) %reduce-scatter.21.cloned.1.call-update) | async-done | bytes 131088 | tf_op jit(solution)/shard_map/reduce_scatter | solution.py:45
  1203.0 2.9 fusion.10
  1206.0 39.8 %psum.70 = f32[2,7]{1,0:T(2,128)S(1)} all-reduce(f32[2,7]{1,0:T(2,128)S(1)} %bitcast.729), channel_id=1, replica_groups=mesh['row'=4,'col'=8] {'row','col'}, use_global_device_ids=true, to_apply=%region_32.34 | all-reduce | flops 14 | bytes 112 | tf_op jit(solution)/shard_map/psum | solution.py:72
  1247.7 39.2 %all-reduce.7 = f32[64]{0:T(128)S(1)} all-reduce(f32[64]{0:T(128)S(1)} %dynamic-update-slice.54), channel_id=8, replica_groups=mesh['row'=4,'col'=8] {'row','col'}, use_global_device_ids=true, to_apply=%add.7 | all-reduce | flops 64 | bytes 512
  1287.3 8.2 all_gather.93
  1296.2 15.5 %convolution_bitcast_fusion = f32[2,128,128]{2,0,1:T(2,128)S(1)} fusion(f32[128,128,128]{2,1,0:T(8,128)} %param.39, f32[128,2,128]{2,1,0:T(2,128)S(1)} %gather_fusion.7, pred[128]{0:T(512)(128)(4,1)S(1)} %compare_and_fusion), kind=kOutput, calls=%fused_computation.12 | convolution fusion | flops 50364416 | bytes 8650880 | tf_op jit(solution)/shard_map/kij,nkj->nki/dot_general | solution.py:44
  1311.6 1.6 fusion.23
  1320.6 2.0 broadcast_select_fusion.5
  1324.1 2.0 broadcast_select_fusion.4
  1327.7 1.9 broadcast_select_fusion.3
  1331.0 1.9 broadcast_select_fusion.2
  1334.4 1.9 broadcast_select_fusion.1
  1337.6 38.8 %reduce-scatter.23.cloned.1.call-done = f32[128,2,128]{2,0,1:T(8,128)} async-done(((f32[1024,2,128]{2,0,1:T(8,128)}), f32[128,2,128]{2,0,1:T(8,128)}) %reduce-scatter.23.cloned.1.call-update) | async-done | bytes 131088 | tf_op jit(solution)/shard_map/reduce_scatter | solution.py:45
  1377.5 3.0 fusion.16
  1380.5 40.1 %psum.71 = f32[2,8]{1,0:T(2,128)S(1)} all-reduce(f32[2,8]{1,0:T(2,128)S(1)} %bitcast.726), channel_id=1, replica_groups=mesh['row'=4,'col'=8] {'row','col'}, use_global_device_ids=true, to_apply=%region_37.39 | all-reduce | flops 16 | bytes 128 | tf_op jit(solution)/shard_map/psum | solution.py:72
  1423.6 39.2 %all-reduce.8 = f32[64]{0:T(128)S(1)} all-reduce(f32[64]{0:T(128)S(1)} %dynamic-update-slice.55), channel_id=9, replica_groups=mesh['row'=4,'col'=8] {'row','col'}, use_global_device_ids=true, to_apply=%add.8 | all-reduce | flops 64 | bytes 512
  1463.0 1.7 broadcast_select_fusion
  (203 shorter events, 76.1 us)
Async XLA Ops:
  7.2 69.7 %copy-start.9 = (s32[1,128]{1,0:T(1,128)S(1)}, s32[1,128]{1,0:T(1,128)}, u32[]{:S(2)}) copy-start(s32[1,128]{1,0:T(1,128)} %param.40) | copy-start | bytes 1540
  7.2 134.6 %copy-start = (f32[16384]{0:T(1024)S(1)}, f32[16384]{0:T(1024)}, u32[]{:S(2)}) copy-start(f32[16384]{0:T(1024)} %param.42) | copy-start | bytes 196612
  7.2 134.6 %reduce-scatter.9.cloned.1.call-start = ((), (), s32[]{:S(2)}) async-start(), calls=%async_computation.8 | async-start | bytes 1179648 | tf_op jit(solution)/shard_map/reduce_scatter | solution.py:45
  78.5 234.6 %reduce-scatter.11.cloned.1.call-start = ((), (), s32[]{:S(2)}) async-start(), calls=%async_computation.9 | async-start | bytes 1179648 | tf_op jit(solution)/shard_map/reduce_scatter | solution.py:45
  249.8 238.0 %reduce-scatter.13.cloned.1.call-start = ((), (), s32[]{:S(2)}) async-start(), calls=%async_computation.10 | async-start | bytes 1179648 | tf_op jit(solution)/shard_map/reduce_scatter | solution.py:45
  424.4 240.1 %reduce-scatter.15.cloned.1.call-start = ((), (), s32[]{:S(2)}) async-start(), calls=%async_computation.11 | async-start | bytes 1179648 | tf_op jit(solution)/shard_map/reduce_scatter | solution.py:45
  532.2 0.7 copy-start.6
  573.8 28.3 %copy-start.2 = (f32[2,16384]{1,0:T(2,128)}, f32[2,16384]{1,0:T(2,128)S(1)}, u32[]{:S(2)}) copy-start(f32[2,16384]{1,0:T(2,128)S(1)} %get-tuple-element.259) | copy-start | bytes 393220
  601.2 247.5 %reduce-scatter.17.cloned.1.call-start = ((), (), s32[]{:S(2)}) async-start(), calls=%async_computation.12 | async-start | bytes 1179648 | tf_op jit(solution)/shard_map/reduce_scatter | solution.py:45
  603.1 182.7 %copy-start.1 = (f32[7,2,16384]{2,1,0:T(2,128)S(1)}, f32[7,2,16384]{2,1,0:T(2,128)}, u32[]{:S(2)}) copy-start(f32[7,2,16384]{2,1,0:T(2,128)} %get-tuple-element.273) | copy-start | bytes 2752516
  665.6 0.7 copy-start.5
  711.9 0.6 copy-start.7
  756.7 0.7 copy-start.3
  785.7 241.8 %reduce-scatter.19.cloned.1.call-start = ((), (), s32[]{:S(2)}) async-start(), calls=%async_computation.13 | async-start | bytes 1179648 | tf_op jit(solution)/shard_map/reduce_scatter | solution.py:45
  849.9 0.7 copy-start.4
  894.3 0.6 copy-start.8
  964.3 237.7 %reduce-scatter.21.cloned.1.call-start = ((), (), s32[]{:S(2)}) async-start(), calls=%async_computation.14 | async-start | bytes 1179648 | tf_op jit(solution)/shard_map/reduce_scatter | solution.py:45
  1138.6 175.9 %copy-start.17 = (s32[3]{0:T(128)S(1)}, s32[3]{0:T(128)}, u32[]{:S(2)}) copy-start(s32[3]{0:T(128)} %constant.460.clone.1) | copy-start | bytes 40
  1138.6 176.6 %copy-start.16 = (s32[3]{0:T(128)S(1)}, s32[3]{0:T(128)}, u32[]{:S(2)}) copy-start(s32[3]{0:T(128)} %constant.463.clone.1) | copy-start | bytes 40
  1138.6 177.3 %copy-start.15 = (s32[3]{0:T(128)S(1)}, s32[3]{0:T(128)}, u32[]{:S(2)}) copy-start(s32[3]{0:T(128)} %constant.465.clone.1) | copy-start | bytes 40
  1138.6 178.1 %copy-start.14 = (s32[3]{0:T(128)S(1)}, s32[3]{0:T(128)}, u32[]{:S(2)}) copy-start(s32[3]{0:T(128)} %constant.467.clone.1) | copy-start | bytes 40
  1138.6 178.9 %copy-start.13 = (s32[3]{0:T(128)S(1)}, s32[3]{0:T(128)}, u32[]{:S(2)}) copy-start(s32[3]{0:T(128)} %constant.469.clone.1) | copy-start | bytes 40
  1138.7 179.6 %copy-start.12 = (s32[3]{0:T(128)S(1)}, s32[3]{0:T(128)}, u32[]{:S(2)}) copy-start(s32[3]{0:T(128)} %constant.471.clone.1) | copy-start | bytes 40
  1138.7 188.9 %copy-start.10 = (f32[2,1,1]{0,2,1:T(1,128)S(1)}, f32[2,1,1]{0,2,1:T(1,128)}, u32[]{:S(2)}) copy-start(f32[2,1,1]{0,2,1:T(1,128)} %get-tuple-element.300) | copy-start | bytes 28
  1138.7 192.2 %copy-start.11 = (f32[2,1,1]{0,2,1:T(1,128)S(1)}, f32[2,1,1]{0,2,1:T(1,128)}, u32[]{:S(2)}) copy-start(f32[2,1,1]{0,2,1:T(1,128)} %get-tuple-element.296) | copy-start | bytes 28
  1138.7 237.7 %reduce-scatter.23.cloned.1.call-start = ((), (), s32[]{:S(2)}) async-start(), calls=%async_computation.15 | async-start | bytes 1179648 | tf_op jit(solution)/shard_map/reduce_scatter | solution.py:45
Sparse Core Ops, SparseCore 0:
  78.6 63.1 reduce-scatter.8
  249.9 63.1 reduce-scatter.10
  424.5 63.1 reduce-scatter.12
  601.3 63.1 reduce-scatter.14
  785.9 62.8 reduce-scatter.16
  964.4 63.0 reduce-scatter.18
  1138.8 63.0 reduce-scatter.20
  1313.4 63.0 reduce-scatter.22
